TPU v7x, 32 devices: a whole 2x2x4 slice. The times are simulated.
32 devices in a mesh: rows: 8 (over z, x), cols: 4 (over y, core).
Axes of the slice: x: 2, y: 2, z: 4, core: 2. Of those that a mesh axis runs over, the one named last changes fastest.
Arguments:
- basis: bfloat16 [65536, 512], P('rows', 'cols'), may hold values from -6 to 6
- lower: bfloat16 [256, 256, 256], P('rows'), may hold values from -0.375 to 0.375
- diag: bfloat16 [256, 256, 256], P('rows'), may hold values from -0.375 to 0.375
- upper: bfloat16 [256, 256, 256], P('rows'), may hold values from -0.375 to 0.375
- inverse: bfloat16 [256, 256, 256], P('rows'), may hold values from -0.375 to 0.375
Outputs:
- ortho: bfloat16 [65536, 512], P('rows', 'cols')
- projected: float32 [512, 512], P(None, 'cols')
All inputs are finite; a program needn't handle non-finite values.
Results may differ from a plain program's by a relative error of at most 0.0085.
Values may be sent and summed in bfloat16 or wider, within the bound.
A program may use at most 128 MiB of HBM per device.

v0:
```python
import jax
import jax.numpy as jnp
from jax import lax
from jax.sharding import PartitionSpec as P


def extended(block, sides, width):
    for axis, dim in sides:
        count = lax.axis_size(axis)
        forward = [(i, i + 1) for i in range(count - 1)]
        backward = [(target, source) for source, target in forward]
        low = lax.ppermute(
            lax.slice_in_dim(block, block.shape[dim] - width, None, axis=dim), axis, forward
        )
        high = lax.ppermute(lax.slice_in_dim(block, 0, width, axis=dim), axis, backward)
        block = jnp.concatenate([low, block, high], axis=dim)
    return block


def inner(left, right):
    return lax.dot_general(
        left, right, (((0,), (0,)), ((), ())), preferred_element_type=jnp.float32
    )


def apply_blocks(padded, lower, diag, upper, inverse):
    count = diag.shape[0]
    size = diag.shape[1]
    width = padded.shape[1]
    blocks = padded.reshape(count + 2, size, width)
    mixed = jnp.einsum("bij,bjc->bic", lower, blocks[:-2], preferred_element_type=jnp.float32)
    mixed = mixed + jnp.einsum(
        "bij,bjc->bic", diag, blocks[1:-1], preferred_element_type=jnp.float32
    )
    mixed = mixed + jnp.einsum(
        "bij,bjc->bic", upper, blocks[2:], preferred_element_type=jnp.float32
    )
    mixed = mixed.astype(jnp.bfloat16)
    result = jnp.einsum("bij,bjc->bic", inverse, mixed, preferred_element_type=jnp.float32)
    return result.astype(jnp.bfloat16).reshape(count * size, width)


def inverse_upper(gram):
    factor = jnp.linalg.cholesky(gram)
    identity = jnp.eye(gram.shape[0], dtype=jnp.float32)
    linv = lax.linalg.triangular_solve(factor, identity, left_side=True, lower=True)
    return linv.T.astype(jnp.bfloat16)


def shards(basis, lower, diag, upper, inverse):
    size = diag.shape[1]
    width = basis.shape[1]

    def operate(field):
        padded = extended(field, (("rows", 0),), size)
        return apply_blocks(padded, lower, diag, upper, inverse)

    work = operate(basis)
    wide = lax.all_gather(work, "cols", axis=1, tiled=True)
    gram = lax.psum(inner(wide, wide), "rows")
    rinv = inverse_upper(gram)
    start = lax.axis_index("cols") * width
    ortho_all = jnp.dot(wide, rinv, preferred_element_type=jnp.float32).astype(jnp.bfloat16)
    ortho = lax.dynamic_slice_in_dim(ortho_all, start, width, 1)
    image = operate(ortho)
    projected = lax.psum(inner(ortho_all, image), "rows")
    return (ortho, projected)


def solution(mesh):
    in_specs = (
        P("rows", "cols"),
        P("rows", None, None),
        P("rows", None, None),
        P("rows", None, None),
        P("rows", None, None),
    )
    out_specs = (P("rows", "cols"), P(None, "cols"))
    return jax.shard_map(shards, mesh=mesh, in_specs=in_specs, out_specs=out_specs, check_vma=False)
```

profile of v0, /device:TPU:0, one launch (start us, length us, event | category | flops | bytes accessed | tf_op | source)
XLA Modules:
  0.0 457.6 jit_solution(3944854083608453380)
XLA Ops:
  7.2 0.9 fusion.44
  8.1 1.3 collective-permute-start.1
  9.4 5.5 %collective-permute-start = (bf16[256,128]{1,0:T(8,128)(2,1)S(1)}, bf16[256,128]{1,0:T(8,128)(2,1)S(1)}, u32[]{:S(2)}, u32[]{:S(2)}) collective-permute-start(bf16[256,128]{1,0:T(8,128)(2,1)S(1)} %get-tuple-element.27), channel_id=1, source_target_pairs={{0,4},{4,8},{8,12},{12,16},{16,20},{20,24},{24,28},{1,5},{5,9},{9,... | collective-permute-start | bytes 196616 | tf_op jit(solution)/shard_map/ppermute | solution.py:12
  14.9 6.5 %fusion.49 = f32[32,256,128]{1,2,0:T(8,128)} fusion(bf16[32,256,256]{2,1,0:T(8,128)(2,1)} %param.7, bf16[32,256,128]{2,1,0:T(8,128)(2,1)} %bitcast.98), kind=kOutput, calls=%fused_computation.97 | convolution fusion | flops 536870912 | bytes 10485760 | tf_op jit(solution)/shard_map/bij,bjc->bic/dot_general | solution.py:32
  21.7 1.9 copy-done.2
  23.6 3.5 fusion.48
  27.0 10.1 %convert_bitcast_fusion.1 = bf16[32,256,128]{1,2,0:T(8,128)(2,1)} fusion(bf16[32,256,256]{2,1,0:T(8,128)(2,1)} %param.9, f32[32,256,128]{1,2,0:T(8,128)} %fusion.49, f32[32,128,256]{2,1,0:T(8,128)} %fusion.48, bf16[32,256,128]{2,1,0:T(8,128)(2,1)S(1)} %bitcast.99, bf16[32,256,256]{2,1,0:T(8,128)(2,1)} %param.8), kind=kOutput, calls=%fused_computation.14 | convolution fusion | flops 1077936128 | bytes 20971520 | tf_op jit(solution)/shard_map/bij,bjc->bic/dot_general | solution.py:39
  37.1 4.0 copy.9
  41.2 61.1 %all-gather.2.cloned.1.call-done = bf16[8192,512]{1,0:T(8,128)(2,1)} async-done(((bf16[8192,128]{1,0:T(8,128)(2,1)}), bf16[8192,512]{1,0:T(8,128)(2,1)}) %all-gather.2.cloned.1.call-update) | async-done | bytes 8388624 | tf_op jit(solution)/shard_map/all_gather | solution.py:59
  102.4 11.3 %fusion.50 = f32[512,512]{0,1:T(8,128)} fusion(bf16[8192,512]{1,0:T(8,128)(2,1)} %all-gather.2.cloned.1.call-done), kind=kOutput, calls=%fused_computation.98 | convolution fusion | flops 4294967296 | bytes 9437184 | tf_op jit(solution)/shard_map/dot_general | solution.py:21
  114.2 0.8 iota_compare_fusion
  115.1 76.9 %all-reduce.4.cloned.1.call-done = f32[512,512]{0,1:T(8,128)} async-done(((f32[512,512]{0,1:T(8,128)}), f32[512,512]{0,1:T(8,128)}) %all-reduce.4.cloned.1.call-update) | async-done | bytes 1048592 | tf_op jit(solution)/shard_map/psum | solution.py:60
  192.0 1.6 copy.11
  193.6 1.4 fusion.4
  195.1 11.7 %cholesky.104 = f32[128,128]{1,0:T(8,128)S(1)} custom-call(f32[128,128]{1,0:T(8,128)S(1)} %cholesky.266), custom_call_target="Cholesky" | custom-call | tf_op jit(solution)/shard_map/jit(cholesky)/cholesky | solution.py:44
  206.8 9.8 %custom-call.30 = f32[1,128,128]{1,2,0:T(8,128)S(1)} custom-call(f32[1,128,128]{2,1,0:T(8,128)S(1)} %get-tuple-element.37), custom_call_target="InvertDiagBlocksLowerTriangular" | custom-call | tf_op jit(solution)/shard_map/jit(cholesky)/cholesky | solution.py:44
  217.4 11.7 %cholesky.217 = f32[128,128]{1,0:T(8,128)S(1)} custom-call(f32[128,128]{1,0:T(8,128)S(1)} %cholesky.270), custom_call_target="Cholesky" | custom-call | tf_op jit(solution)/shard_map/jit(cholesky)/cholesky | solution.py:44
  229.2 9.9 %custom-call.31 = f32[1,128,128]{1,2,0:T(8,128)S(1)} custom-call(f32[1,128,128]{2,1,0:T(8,128)S(1)} %get-tuple-element.34), custom_call_target="InvertDiagBlocksLowerTriangular" | custom-call | tf_op jit(solution)/shard_map/jit(cholesky)/cholesky | solution.py:44
  239.8 11.7 %cholesky.238 = f32[128,128]{1,0:T(8,128)S(1)} custom-call(f32[128,128]{1,0:T(8,128)S(1)} %cholesky.275), custom_call_target="Cholesky" | custom-call | tf_op jit(solution)/shard_map/jit(cholesky)/cholesky | solution.py:44
  251.6 0.7 compare_reduce_fusion.1
  252.3 9.8 %custom-call.32 = f32[1,128,128]{1,2,0:T(8,128)S(1)} custom-call(f32[1,128,128]{2,1,0:T(8,128)S(1)} %get-tuple-element.31), custom_call_target="InvertDiagBlocksLowerTriangular" | custom-call | tf_op jit(solution)/shard_map/jit(cholesky)/cholesky | solution.py:44
  262.7 11.7 %cholesky.255 = f32[128,128]{1,0:T(8,128)S(1)} custom-call(f32[128,128]{1,0:T(8,128)S(1)} %convolution_subtract_fusion.5), custom_call_target="Cholesky" | custom-call | tf_op jit(solution)/shard_map/jit(cholesky)/cholesky | solution.py:44
  274.4 0.7 compare_reduce_fusion
  275.1 0.8 compare_reduce_fusion.2
  278.7 10.8 %while.1 = (s32[]{:T(128)}, f32[512,512]{1,0:T(8,128)S(1)}, s32[4,2]{0,1:T(2,128)S(1)}, f32[4,128,128]{2,1,0:T(8,128)}, s32[]{:T(128)}) while((s32[]{:T(128)}, f32[512,512]{1,0:T(8,128)S(1)}, s32[4,2]{0,1:T(2,128)S(1)}, f32[4,128,128]{2,1,0:T(8,128)}, s32[]{:T(128)}) %tuple.38), condition=%wide.while_cond, body=%wide.while_body.sunk | while | flops 2 | bytes 132205 | solution.py:46
  278.8 0.6 fusion.79
  279.4 2.0 bitcast_dynamic-update-slice_fusion.2
  281.5 0.6 fusion.79
  282.1 2.0 bitcast_dynamic-update-slice_fusion.2
  284.2 0.6 fusion.79
  284.8 2.0 bitcast_dynamic-update-slice_fusion.2
  286.9 0.6 fusion.79
  287.5 2.1 bitcast_dynamic-update-slice_fusion.2
  289.5 40.1 %custom-call.33 = f32[4,128,128]{1,2,0:T(8,128)S(1)} custom-call(f32[4,128,128]{2,1,0:T(8,128)} %get-tuple-element.9), custom_call_target="InvertDiagBlocksLowerTriangular" | custom-call | tf_op jit(solution)/shard_map/triangular_solve | solution.py:46
  329.6 1.1 fusion.47
  332.4 0.6 convolution_subtract_fusion.2
  333.5 8.8 %convolution_convert_fusion = bf16[8192,512]{1,0:T(8,128)(2,1)S(1)} fusion(bf16[8192,512]{1,0:T(8,128)(2,1)} %all-gather.2.cloned.1.call-done, bf16[128,512]{1,0:T(8,128)(2,1)S(1)} %convolution_convert_fusion.1, bf16[128,512]{1,0:T(8,128)(2,1)S(1)} %get-tuple-element.40, bf16[128,512]{1,0:T(8,128)(2,1)S(1)} %get-tuple-element.42, ...), kind=kOutput, calls=%fused_computation.2 | convolution fusion | flops 4301258752 | bytes 17301504 | tf_op jit(solution)/shard_map/dot_general | solution.py:63
  342.7 3.6 collective-permute-start.2
  346.2 1.7 collective-permute-start.3
  347.9 3.4 fusion.51
  351.4 1.1 collective-permute-done.3
  352.8 0.8 copy-done.1
  353.6 3.5 fusion.52
  357.0 10.1 %convert_bitcast_fusion = bf16[32,256,128]{1,2,0:T(8,128)(2,1)} fusion(bf16[32,256,256]{2,1,0:T(8,128)(2,1)} %param.9, f32[32,128,256]{2,1,0:T(8,128)} %fusion.52, f32[32,128,256]{2,1,0:T(8,128)} %fusion.51, bf16[32,256,128]{2,1,0:T(8,128)(2,1)S(1)} %bitcast.100, bf16[32,256,256]{2,1,0:T(8,128)(2,1)} %param.6), kind=kOutput, calls=%fused_computation.13 | convolution fusion | flops 1077936128 | bytes 20971520 | tf_op jit(solution)/shard_map/bij,bjc->bic/dot_general | solution.py:39
  367.1 3.2 copy.12
  370.3 6.4 %fusion.53 = f32[512,128]{1,0:T(8,128)} fusion(bf16[8192,512]{1,0:T(8,128)(2,1)} %copy-done.5, bf16[8192,128]{1,0:T(8,128)(2,1)S(1)} %bitcast.104), kind=kOutput, calls=%fused_computation.101 | convolution fusion | flops 1073741824 | bytes 10747904 | tf_op jit(solution)/shard_map/dot_general | solution.py:21
  376.8 72.2 %all-reduce.6.cloned.1.call-done = f32[512,128]{1,0:T(8,128)} async-done(((f32[512,128]{1,0:T(8,128)}), f32[512,128]{1,0:T(8,128)}) %all-reduce.6.cloned.1.call-update) | async-done | bytes 262160 | tf_op jit(solution)/shard_map/psum | solution.py:66
  449.0 1.7 copy.31
  (51 shorter events, 6.3 us)
Async XLA Ops:
  7.2 95.2 %all-gather.2.cloned.1.call-start = ((), (), s32[]{:S(2)}) async-start(), calls=%async_computation | async-start | bytes 10485760 | tf_op jit(solution)/shard_map/all_gather | solution.py:59
  8.1 13.3 %collective-permute-start.1 = (bf16[256,128]{1,0:T(8,128)(2,1)S(1)}, bf16[256,128]{1,0:T(8,128)(2,1)S(1)}, u32[]{:S(2)}, u32[]{:S(2)}) collective-permute-start(bf16[256,128]{1,0:T(8,128)(2,1)S(1)} %get-tuple-element.26), channel_id=1, source_target_pairs={{4,0},{8,4},{12,8},{16,12},{20,16},{24,20},{28,24},{5,1},{9,5},{13... | collective-permute-start | bytes 196616 | tf_op jit(solution)/shard_map/ppermute | solution.py:15
  9.4 12.0 %collective-permute-start = (bf16[256,128]{1,0:T(8,128)(2,1)S(1)}, bf16[256,128]{1,0:T(8,128)(2,1)S(1)}, u32[]{:S(2)}, u32[]{:S(2)}) collective-permute-start(bf16[256,128]{1,0:T(8,128)(2,1)S(1)} %get-tuple-element.27), channel_id=1, source_target_pairs={{0,4},{4,8},{8,12},{12,16},{16,20},{20,24},{24,28},{1,5},{5,9},{9,... | collective-permute-start | bytes 196616 | tf_op jit(solution)/shard_map/ppermute | solution.py:12
  14.9 6.5 %copy-start.4 = (bf16[8192,128]{1,0:T(8,128)(2,1)S(1)}, bf16[8192,128]{1,0:T(8,128)(2,1)}, u32[]{:S(2)}) copy-start(bf16[8192,128]{1,0:T(8,128)(2,1)} %param.5) | copy-start | bytes 6291460
  21.4 2.2 copy-start.2
  41.2 150.9 %all-reduce.4.cloned.1.call-start = ((), (), s32[]{:S(2)}) async-start(), calls=%async_computation.1 | async-start | bytes 2097152 | tf_op jit(solution)/shard_map/psum | solution.py:60
  113.7 335.3 %all-reduce.6.cloned.1.call-start = ((), (), s32[]{:S(2)}) async-start(), calls=%async_computation.2 | async-start | bytes 524288 | tf_op jit(solution)/shard_map/psum | solution.py:66
  342.3 9.1 %copy-start.5 = (bf16[8192,512]{1,0:T(8,128)(2,1)}, bf16[8192,512]{1,0:T(8,128)(2,1)S(1)}, u32[]{:S(2)}) copy-start(bf16[8192,512]{1,0:T(8,128)(2,1)S(1)} %convolution_convert_fusion) | copy-start | bytes 25165828
  342.3 5.6 %copy-start.3 = (bf16[32,256,256]{2,1,0:T(8,128)(2,1)S(1)}, bf16[32,256,256]{2,1,0:T(8,128)(2,1)}, u32[]{:S(2)}) copy-start(bf16[32,256,256]{2,1,0:T(8,128)(2,1)} %param.7) | copy-start | bytes 12582916
  342.6 9.9 %copy-start = (bf16[8192,128]{1,0:T(8,128)(2,1)}, bf16[8192,128]{1,0:T(8,128)(2,1)S(1)}, u32[]{:S(2)}) copy-start(bf16[8192,128]{1,0:T(8,128)(2,1)S(1)} %constant_dynamic-slice_fusion.2) | copy-start | bytes 6291460
  342.7 8.7 %collective-permute-start.2 = (bf16[256,128]{1,0:T(8,128)(2,1)S(1)}, bf16[256,128]{1,0:T(8,128)(2,1)S(1)}, u32[]{:S(2)}, u32[]{:S(2)}) collective-permute-start(bf16[256,128]{1,0:T(8,128)(2,1)S(1)} %get-tuple-element.20), channel_id=1, source_target_pairs={{0,4},{4,8},{8,12},{12,16},{16,20},{20,24},{24,28},{1,5},{5,9},{9,... | collective-permute-start | bytes 196616 | tf_op jit(solution)/shard_map/ppermute | solution.py:12
  346.2 6.3 %collective-permute-start.3 = (bf16[256,128]{1,0:T(8,128)(2,1)S(1)}, bf16[256,128]{1,0:T(8,128)(2,1)S(1)}, u32[]{:S(2)}, u32[]{:S(2)}) collective-permute-start(bf16[256,128]{1,0:T(8,128)(2,1)S(1)} %get-tuple-element.21), channel_id=1, source_target_pairs={{4,0},{8,4},{12,8},{16,12},{20,16},{24,20},{28,24},{5,1},{9,5},{13... | collective-permute-start | bytes 196616 | tf_op jit(solution)/shard_map/ppermute | solution.py:15
  351.4 2.2 copy-start.1
Sparse Core Ops, SparseCore 0:
  41.3 61.0 all-gather.1
  113.8 78.2 all-reduce.3
  376.9 72.0 all-reduce.5
where the time goes:
time: 465 us; the launch traced here: 458 us
  waiting for transfers between devices  211 us (45%)
  other arithmetic  122 us (26%)
  matrix products  69.2 us (15%)
  local copies, waits for them, and re-layouts  25.3 us (5%)
  between operations  17.1 us (4%)
  starting transfers between devices  12.6 us (3%)
    another operation x14, other arithmetic, inverse_upper(): factor = jnp.linalg.cholesky(gram)  78.8 us
    psum x1, waiting for transfers between devices, shards(): gram = lax.psum(inner(wide, wide), 'rows')  76.9 us
    psum x1, waiting for transfers between devices, shards(): projected = lax.psum(inner(ortho_all, image), 'rows')  72.2 us
    all_gather x1, waiting for transfers between devices, shards(): wide = lax.all_gather(work, 'cols', axis=1, tiled=True)  61.1 us
    another operation x3, other arithmetic, inverse_upper(): lax.linalg.triangular_solve(factor, identity, left_side=True, lower=True)  40.3 us
    dot_general x2, matrix products, apply_blocks(): jnp.einsum('bij,bjc->bic', inverse, mixed, preferred_element_type=jnp.flo...  20.1 us
    dot_general x2, matrix products, inner(): lax.dot_general(left, right, (((0,), (0,)), ((), ())), preferred_element_...  17.7 us
    another operation x12, local copies, waits for them, and re-layouts  10.8 us
  transfers between devices with their start and end apart: 7, of which 4 were waited for; matrix products, arithmetic and copies ran while one was open for 2% of the time, Pallas kernels for 0%

commit v1 on v0

v1 whole, which is shorter than its diff:
```python
import functools

import jax
import jax.numpy as jnp
from jax import lax
from jax.experimental import pallas as pl
from jax.experimental.pallas import tpu as pltpu
from jax.sharding import PartitionSpec as P

LANES = 128
MESH = pl.DeviceIdType.MESH
VMEM = pl.BlockSpec(memory_space=pltpu.VMEM)
ANY = pl.BlockSpec(memory_space=pl.ANY)
SUB = 8
HI = lax.Precision.HIGHEST

def factor_tile(block):
    size = block.shape[0]
    wide = (SUB, size)
    tiles = size // SUB
    row_of = lax.broadcasted_iota(jnp.int32, wide, 0)
    lane_of = lax.broadcasted_iota(jnp.int32, wide, 1)
    a = [block[t * SUB:(t + 1) * SUB, :] for t in range(tiles)]
    m = [jnp.where(lane_of == row_of + t * SUB, 1.0, 0.0).astype(jnp.float32) for t in range(tiles)]
    out = []
    for t in range(tiles):
        at, mt = a[t], m[t]
        base = t * SUB
        pivot = {}
        for i in range(SUB):
            for j in range(i + 1):
                pivot[i, j] = jnp.broadcast_to(at[i:i + 1, base + j:base + j + 1], wide)
        ra = [jnp.broadcast_to(at[i:i + 1, :], wide) for i in range(SUB)]
        rm = [jnp.broadcast_to(mt[i:i + 1, :], wide) for i in range(SUB)]
        last = t == tiles - 1
        unit = {}
        sa, sm = [None] * SUB, [None] * SUB
        fin = jnp.zeros(wide, jnp.float32)
        for j in range(SUB):
            d = pivot[j, j]
            root = lax.rsqrt(d)
            inv = 1.0 / d
            fin = jnp.where(row_of == j, rm[j] * root, fin)
            for i in range(j + 1, SUB):
                unit[i, j] = pivot[i, j] * inv
            for i in range(j + 1, SUB):
                for q in range(j + 1, i + 1):
                    pivot[i, q] = pivot[i, q] - unit[i, j] * pivot[q, j]
            for i in range(j + 1, SUB):
                if not last:
                    ra[i] = ra[i] - unit[i, j] * ra[j]
                rm[i] = rm[i] - unit[i, j] * rm[j]
            if not last:
                sa[j] = ra[j] * inv
                sm[j] = rm[j] * inv
        out.append(fin)
        if last:
            break
        for j in range(SUB - 1, -1, -1):
            for i in range(j):
                sa[i] = sa[i] - unit[j, i] * sa[j]
                sm[i] = sm[i] - unit[j, i] * sm[j]
        for s in range(t + 1, tiles):
            na, nm = a[s], m[s]
            for j in range(SUB):
                c = jnp.broadcast_to(a[s][:, base + j:base + j + 1], wide)
                na = na - c * sa[j]
                nm = nm - c * sm[j]
            a[s], m[s] = na, nm
    return jnp.concatenate(out, axis=0)

def inverse_upper_steps(work_ref, out_ref, panel_ref):
    n, size, _ = work_ref.shape
    order = n * size
    def step(b, carry):
        at = [work_ref[b, :, i * size:(i + 1) * size] for i in range(n)]
        block = at[0]
        for i in range(1, n):
            block = jnp.where(b == i, at[i], block)
        linv = factor_tile(block)
        y = lax.dot_general(linv, work_ref[b], (((1,), (0,)), ((), ())), precision=HI, preferred_element_type=jnp.float32)
        work_ref[b] = y
        for i in range(n):
            panel_ref[i] = y[:, i * size:(i + 1) * size]
        def below(i, c):
            work_ref[i] = work_ref[i] - lax.dot_general(panel_ref[i], y_ref[...], (((0,), (0,)), ((), ())), precision=HI, preferred_element_type=jnp.float32)
            return c
        y_ref = work_ref.at[b]
        lax.fori_loop(b + 1, n, below, 0)
        return carry
    lax.fori_loop(0, n, step, 0)
    for b in range(n):
        out_ref[:, b * size:(b + 1) * size] = work_ref[b, :, order:].T.astype(out_ref.dtype)

def unpack_kernel(packed_ref, out_ref, work_ref, panel_ref):
    n, size, _ = work_ref.shape
    order = n * size
    row = lax.broadcasted_iota(jnp.int32, (size, order), 0)
    lane = lax.broadcasted_iota(jnp.int32, (size, order), 1)
    place = 0
    for i in range(n):
        work_ref[i, :, :order] = jnp.zeros((size, order), jnp.float32)
        work_ref[i, :, order:] = jnp.where(lane == row + i * size, 1.0, 0.0).astype(jnp.float32)
        for j in range(i, n):
            work_ref[i, :, j * size:(j + 1) * size] = packed_ref[place * size:(place + 1) * size, :]
            place += 1
    inverse_upper_steps(work_ref, out_ref, panel_ref)


def inverse_upper(packed, order):
    n = order // LANES
    return pl.pallas_call(
        unpack_kernel,
        out_shape=jax.ShapeDtypeStruct((order, order), jnp.bfloat16),
        in_specs=[VMEM],
        out_specs=VMEM,
        scratch_shapes=[
            pltpu.VMEM((n, LANES, 2 * order), jnp.float32),
            pltpu.VMEM((n, LANES, LANES), jnp.float32),
        ],
        cost_estimate=pl.CostEstimate(
            flops=8 * order**3, bytes_accessed=8 * order * order, transcendentals=0
        ),
        name="inverse_upper",
    )(packed)


def dot(left, right):
    return jnp.dot(left, right, preferred_element_type=jnp.float32)


def inner(left, right):
    return lax.dot_general(
        left, right, (((0,), (0,)), ((), ())), preferred_element_type=jnp.float32
    )


def remote(src, dst, send, recv, **where):
    return pltpu.make_async_remote_copy(
        src_ref=src, dst_ref=dst, send_sem=send, recv_sem=recv, device_id=where, device_id_type=MESH
    )


def exchange(axis, count, me, source, target, arrived, send, recv):
    for step in range(1, count):
        peer = lax.rem(me + step, count)
        remote(source(peer), target(me), send.at[step], recv.at[me], **{axis: peer}).start()

    def finish():
        for step in range(1, count):
            peer = lax.rem(me + step, count)
            remote(
                source(peer), arrived(peer), send.at[step], recv.at[peer], **{axis: peer}
            ).wait()

    return finish


def apply_block(i, size, field, wl, wd, wu, wi):
    def at(k):
        return field[pl.ds(pl.multiple_of(k * size, size), size), :]

    mixed = dot(wl[i], at(i)) + dot(wd[i], at(i + 1)) + dot(wu[i], at(i + 2))
    return dot(wi[i], mixed.astype(jnp.bfloat16)).astype(jnp.bfloat16)


def fetch_blocks(parts, held, sem, first):
    count = held[0].shape[0]
    copies = [
        pltpu.make_async_copy(part.at[pl.ds(first * count, count)], ref, sem.at[k])
        for k, (part, ref) in enumerate(zip(parts, held))
    ]
    for copy in copies:
        copy.start()
    return copies


def front_kernel(
    nr, nc, basis, lower, diag, upper, inverse, wext, gram,
    field, wl, wd, wu, wi, total, packed, got1, part, got2,
    wsem, lsem, fsend, frecv, hsend, hrecv, s1, r1, s2, r2, s3, r3, s4, r4,
):
    r, c = lax.axis_index("rows"), lax.axis_index("cols")
    count, size, _ = wl.shape
    width = basis.shape[1]
    body = count * size
    top = (count + 1) * size
    share = got1.shape[1]
    piece = got2.shape[1]

    weights = fetch_blocks((lower, diag, upper, inverse), (wl, wd, wu, wi), wsem, c)

    def columns(k):
        return pl.ds(pl.multiple_of(k * width, width), width)

    def rows(start, extent):
        return pl.ds(pl.multiple_of(start, size), extent)

    spans = ((size, body), (0, size), (top, size))

    def landing(kind, k):
        start, extent = spans[kind]
        return field.at[pl.ds(start, extent), columns(k)]

    def leaving(kind, d):
        start, extent = ((d * body, body), (d * body - size, size), (d * body + body, size))[kind]
        return basis.at[rows(start, extent), :]

    def to_peer(step, kind):
        d = lax.rem(c + step, nc)
        return remote(leaving(kind, d), landing(kind, c), fsend.at[kind, step], frecv.at[kind, c], cols=d)

    def own(kind):
        return pltpu.make_async_copy(leaving(kind, c), landing(kind, c), lsem.at[kind])

    def down():
        return remote(
            basis.at[pl.ds(nc * body - size, size), :], landing(1, c), fsend.at[1, 0], frecv.at[1, c],
            rows=r + 1, cols=0,
        )

    def up():
        return remote(
            basis.at[pl.ds(0, size), :], landing(2, c), fsend.at[2, 0], frecv.at[2, c],
            rows=r - 1, cols=nc - 1,
        )

    pl.when(r < nr - 1)(lambda: down().start())
    pl.when(r > 0)(lambda: up().start())
    for step in range(1, nc):
        d = lax.rem(c + step, nc)
        to_peer(step, 0).start()
        pl.when(d > 0)(lambda: to_peer(step, 1).start())
        pl.when(d < nc - 1)(lambda: to_peer(step, 2).start())
    own(0).start()
    pl.when(c > 0)(lambda: own(1).start())
    pl.when(c < nc - 1)(lambda: own(2).start())

    @pl.when((r == 0) & (c == 0))
    def _():
        field[0:size, :] = jnp.zeros((size, field.shape[1]), field.dtype)
        wext[0:size, :] = jnp.zeros((size, field.shape[1]), field.dtype)

    @pl.when((r == nr - 1) & (c == nc - 1))
    def _():
        field[top:top + size, :] = jnp.zeros((size, field.shape[1]), field.dtype)
        wext[top:top + size, :] = jnp.zeros((size, field.shape[1]), field.dtype)

    total[...] = jnp.zeros_like(total)

    def arrive(kind, k):
        start, extent = spans[kind]
        remote(
            basis.at[pl.ds(0, extent), :], landing(kind, k), fsend.at[kind, 0], frecv.at[kind, k], cols=k
        ).wait_recv()

    for copy in weights:
        copy.wait()
    own(0).wait()
    pl.when(c > 0)(lambda: own(1).wait())
    pl.when(c < nc - 1)(lambda: own(2).wait())
    for k in range(nc):
        pl.when(k != c)(lambda: arrive(0, k))
        pl.when(((c > 0) & (k != c)) | ((c == 0) & (r > 0)))(lambda: arrive(1, k))
        pl.when(((c < nc - 1) & (k != c)) | ((c == nc - 1) & (r < nr - 1)))(lambda: arrive(2, k))

    def block(i, carry):
        w = apply_block(i, size, field, wl, wd, wu, wi)
        wext[rows((i + 1) * size, size), :] = w
        total[...] += inner(w, w)
        return carry

    lax.fori_loop(0, count, block, 0)

    flat = r * nc + c
    last = nr * nc - 1

    def halo(kind):
        start = (body, size)[kind]
        target = (0, top)[kind]
        to = flat + (1, -1)[kind]
        return remote(
            wext.at[pl.ds(start, size), :], wext.at[pl.ds(target, size), :], hsend.at[kind], hrecv.at[kind],
            rows=to // nc, cols=lax.rem(to, nc),
        )

    place = 0
    across = total.shape[0] // LANES
    for i in range(across):
        for j in range(i, across):
            packed[place * LANES:(place + 1) * LANES, :] = total[
                i * LANES:(i + 1) * LANES, j * LANES:(j + 1) * LANES
            ]
            place += 1
    spare = packed.shape[0] - place * LANES
    if spare:
        packed[place * LANES:, :] = jnp.zeros((spare, LANES), jnp.float32)

    def tile(ref, start, extent):
        return ref.at[pl.ds(pl.multiple_of(start, 8), extent), :]

    finish = exchange(
        "cols", nc, c, lambda d: tile(packed, d * share, share), lambda k: got1.at[k],
        lambda k: got1.at[k], s1, r1,
    )
    pl.when(flat < last)(lambda: halo(0).start())
    pl.when(flat > 0)(lambda: halo(1).start())
    got1[c] = packed[pl.ds(pl.multiple_of(c * share, 8), share), :]
    finish()
    part[...] = sum((got1[k] for k in range(1, nc)), got1[0])
    finish = exchange(
        "rows", nr, r, lambda d: tile(part, d * piece, piece), lambda k: got2.at[k],
        lambda k: got2.at[k], s2, r2,
    )
    got2[r] = part[pl.ds(pl.multiple_of(r * piece, 8), piece), :]
    finish()
    mine = c * share + r * piece
    gram[pl.ds(pl.multiple_of(mine, 8), piece), :] = sum((got2[k] for k in range(1, nr)), got2[0])
    exchange(
        "rows", nr, r, lambda d: tile(gram, mine, piece), lambda k: tile(gram, mine, piece),
        lambda k: tile(gram, c * share + k * piece, piece), s3, r3,
    )()
    exchange(
        "cols", nc, c, lambda d: tile(gram, c * share, share), lambda k: tile(gram, c * share, share),
        lambda k: tile(gram, k * share, share), s4, r4,
    )()

    pl.when(flat < last)(lambda: halo(0).wait_send())
    pl.when(flat > 0)(lambda: halo(1).wait_send())
    pl.when(flat > 0)(lambda: halo(0).wait_recv())
    pl.when(flat < last)(lambda: halo(1).wait_recv())
    pl.when(r < nr - 1)(lambda: down().wait_send())
    pl.when(r > 0)(lambda: up().wait_send())
    for step in range(1, nc):
        d = lax.rem(c + step, nc)
        to_peer(step, 0).wait_send()
        pl.when(d > 0)(lambda: to_peer(step, 1).wait_send())
        pl.when(d < nc - 1)(lambda: to_peer(step, 2).wait_send())


def back_kernel(
    nr, nc, wext, rinv, lower, diag, upper, inverse, ortho, projected,
    oext, wl, wd, wu, wi, total, got1, part, got2,
    wsem, lsem, osend, orecv, s1, r1, s2, r2, s3, r3,
):
    r, c = lax.axis_index("rows"), lax.axis_index("cols")
    count, size, _ = wl.shape
    width = ortho.shape[1]
    body = count * size
    piece = got2.shape[1]

    weights = fetch_blocks((lower, diag, upper, inverse), (wl, wd, wu, wi), wsem, c)

    def at(i):
        return pl.ds(pl.multiple_of(i * size, size), size)

    def turn(i, carry):
        oext[at(i), :] = dot(wext[at(i), :], rinv[...]).astype(jnp.bfloat16)
        return carry

    lax.fori_loop(0, count + 2, turn, 0)

    def columns(k):
        return oext.at[pl.ds(size, body), pl.ds(pl.multiple_of(k * width, width), width)]

    def home(k):
        return ortho.at[pl.ds(pl.multiple_of(k * body, size), body), :]

    finish_ortho = exchange("cols", nc, c, columns, home, home, osend, orecv)
    own = pltpu.make_async_copy(columns(c), home(c), lsem)
    own.start()
    total[...] = jnp.zeros_like(total)
    for copy in weights:
        copy.wait()

    def block(i, carry):
        image = apply_block(i, size, oext, wl, wd, wu, wi)
        total[...] += inner(oext[at(i + 1), :], image)
        return carry

    lax.fori_loop(0, count, block, 0)

    def slab(k):
        return pl.ds(pl.multiple_of(k * width, width), width)

    finish = exchange(
        "cols", nc, c, lambda d: total.at[:, slab(d)], lambda k: got1.at[k], lambda k: got1.at[k], s1, r1
    )
    got1[c] = total[:, slab(c)]
    finish()
    part[...] = sum((got1[k] for k in range(1, nc)), got1[0])

    def tile(ref, k):
        return ref.at[pl.ds(pl.multiple_of(k * piece, 8), piece), :]

    finish = exchange(
        "rows", nr, r, lambda d: tile(part, d), lambda k: got2.at[k], lambda k: got2.at[k], s2, r2
    )
    got2[r] = part[pl.ds(pl.multiple_of(r * piece, 8), piece), :]
    finish()
    projected[pl.ds(pl.multiple_of(r * piece, 8), piece), :] = sum(
        (got2[k] for k in range(1, nr)), got2[0]
    )
    exchange(
        "rows", nr, r, lambda d: tile(projected, r), lambda k: tile(projected, r),
        lambda k: tile(projected, k), s3, r3,
    )()
    own.wait()
    finish_ortho()


def shards(nr, nc, basis, lower, diag, upper, inverse):
    blocks, size, _ = diag.shape
    width = basis.shape[1]
    order = width * nc
    count = blocks // nc
    across = order // LANES
    tiles = across * (across + 1) // 2 * LANES // 8
    piece = -(-tiles // (nr * nc)) * 8
    share = piece * nr
    dma = pltpu.SemaphoreType.DMA
    held = [pltpu.VMEM((count, size, size), jnp.bfloat16)] * 4
    extended = ((count + 2) * size, order)
    pair = lambda n: [dma((n,)), dma((n,))]
    opflops = 8 * count * size * size * order + 2 * count * size * order * order

    wext, gram = pl.pallas_call(
        functools.partial(front_kernel, nr, nc),
        out_shape=(
            jax.ShapeDtypeStruct(extended, jnp.bfloat16),
            jax.ShapeDtypeStruct((nc * share, LANES), jnp.float32),
        ),
        in_specs=[ANY] * 5,
        out_specs=(VMEM, VMEM),
        scratch_shapes=[pltpu.VMEM(extended, jnp.bfloat16)] + held + [
            pltpu.VMEM((order, order), jnp.float32),
            pltpu.VMEM((nc * share, LANES), jnp.float32),
            pltpu.VMEM((nc, share, LANES), jnp.float32),
            pltpu.VMEM((share, LANES), jnp.float32),
            pltpu.VMEM((nr, piece, LANES), jnp.float32),
            dma((4,)), dma((3,)), dma((3, nc)), dma((3, nc)), dma((2,)), dma((2,)),
        ] + pair(nc) + pair(nr) + pair(nr) + pair(nc),
        compiler_params=pltpu.CompilerParams(has_side_effects=True),
        cost_estimate=pl.CostEstimate(flops=opflops, bytes_accessed=1 << 23, transcendentals=0),
        name="front",
    )(basis, lower, diag, upper, inverse)

    rinv = inverse_upper(gram, order)

    lines = order // nr
    return pl.pallas_call(
        functools.partial(back_kernel, nr, nc),
        out_shape=(
            jax.ShapeDtypeStruct(basis.shape, jnp.bfloat16),
            jax.ShapeDtypeStruct((order, width), jnp.float32),
        ),
        in_specs=[VMEM, VMEM] + [ANY] * 4,
        out_specs=(ANY, VMEM),
        scratch_shapes=[pltpu.VMEM(extended, jnp.bfloat16)] + held + [
            pltpu.VMEM((order, order), jnp.float32),
            pltpu.VMEM((nc, order, width), jnp.float32),
            pltpu.VMEM((order, width), jnp.float32),
            pltpu.VMEM((nr, lines, width), jnp.float32),
            dma((4,)), dma,
        ] + pair(nc) + pair(nc) + pair(nr) + pair(nr),
        compiler_params=pltpu.CompilerParams(has_side_effects=True),
        cost_estimate=pl.CostEstimate(flops=opflops, bytes_accessed=1 << 23, transcendentals=0),
        name="back",
    )(wext, rinv, lower, diag, upper, inverse)


def solution(mesh):
    in_specs = (
        P("rows", "cols"),
        P("rows", None, None),
        P("rows", None, None),
        P("rows", None, None),
        P("rows", None, None),
    )
    out_specs = (P("rows", "cols"), P(None, "cols"))
    body = functools.partial(shards, mesh.shape["rows"], mesh.shape["cols"])
    return jax.shard_map(body, mesh=mesh, in_specs=in_specs, out_specs=out_specs, check_vma=False)
```

time: 465 us -> 168 us (0.36); the launches traced: 458 us -> 168 us
  waiting for transfers between devices: 211 us -> 0 us
  Pallas kernels: 0 us -> 164 us
  other arithmetic: 122 us -> 0 us
  matrix products: 69.2 us -> 0 us
  local copies, waits for them, and re-layouts: 25.3 us -> 3.79 us
  between operations: 17.1 us -> 0.65 us
  starting transfers between devices: 12.6 us -> 0 us
    pallas_call x0 -> x3, Pallas kernels: none -> 164 us  [the longest x1 75.2 us: shards(): pl.pallas_call(functools.partial(front_kernel, nr, nc), out_shape=(jax.Sh...]
    psum x2 -> x0, waiting for transfers between devices: 149 us -> none  [the longest x1 76.9 us: shards(): gram = lax.psum(inner(wide, wide), 'rows')]
    another operation x17 -> x0, other arithmetic: 119 us -> none  [the longest x14 78.8 us: inverse_upper(): factor = jnp.linalg.cholesky(gram)]
    dot_general x9 -> x0, matrix products: 63.5 us -> none  [the longest x2 20.1 us: apply_blocks(): jnp.einsum('bij,bjc->bic', inverse, mixed, preferred_element_type=jnp.flo...]
    all_gather x1 -> x0, waiting for transfers between devices: 61.1 us -> none  [shards(): wide = lax.all_gather(work, 'cols', axis=1, tiled=True)]
    ppermute x4 -> x0, starting transfers between devices: 12.1 us -> none  [the longest x2 9.09 us: extended(): lax.ppermute(lax.slice_in_dim(block, block.shape[dim] - width, None, axis...]
    another operation x17 -> x0, local copies, waits for them, and re-layouts: 10.9 us -> none
    convert_element_type x2 -> x0, local copies, waits for them, and re-layouts: 7.26 us -> none  [apply_blocks(): return result.astype(jnp.bfloat16).reshape(count * size, width)]
  transfers between devices with their start and end apart: 7 -> 0, of which waited for: 4 -> 0; matrix products, arithmetic and copies ran while one was open for 2% -> 0% of each run, Pallas kernels for 0% -> 0%
where the time goes in v1:
time: 168 us
  Pallas kernels  164 us (98%)
  local copies, waits for them, and re-layouts  3.79 us (2%)
    pallas_call x1, Pallas kernels, shards(): pl.pallas_call(functools.partial(front_kernel, nr, nc), out_shape=(jax.Sh...  75.2 us
    pallas_call x1, Pallas kernels, shards(): pl.pallas_call(functools.partial(back_kernel, nr, nc), out_shape=(jax.Sha...  60 us
    pallas_call x1, Pallas kernels, inverse_upper(): pl.pallas_call(unpack_kernel, out_shape=jax.ShapeDtypeStruct((order, orde...  28.6 us
    unnamed x4, local copies, waits for them, and re-layouts  3.79 us

profile of v1, /device:TPU:0, one launch (start us, length us, event | category | flops | bytes accessed | tf_op | source)
XLA Modules:
  0.0 168.2 jit_solution(4851346552107101414)
XLA Ops:
  0.6 75.2 %front.1 = (bf16[2560,512]{1,0:T(8,128)(2,1)}, f32[1280,128]{1,0:T(8,128)}) custom-call(bf16[8192,128]{1,0:T(8,128)(2,1)} %basis.1, bf16[32,256,256]{2,1,0:T(8,128)(2,1)} %lower.3, bf16[32,256,256]{2,1,0:T(8,128)(2,1)} %diag.3, bf16[32,256,256]{2,1,0:T(8,128)(2,1)} %upper.3, bf16[32,256,256]{2,1,0:T(8,128)(2,1)} %inverse.3), custom_call_target="tpu_custom_call" | custom-call | flops 3221225472 | bytes 8388608 | tf_op jit(solution)/shard_map/front/pallas_call | solution.py:427
  75.8 28.6 %inverse_upper.1.rinv = bf16[512,512]{1,0:T(8,128)(2,1)} custom-call(f32[1280,128]{1,0:T(8,128)} %get-tuple-element.5.packed_ref), custom_call_target="tpu_custom_call" | custom-call | flops 1073741824 | bytes 2097152 | tf_op jit(solution)/shard_map/inverse_upper/pallas_call | solution.py:112
  104.4 60.0 %back.1 = (bf16[8192,128]{1,0:T(8,128)(2,1)}, f32[512,128]{1,0:T(8,128)}) custom-call(bf16[2560,512]{1,0:T(8,128)(2,1)} %get-tuple-element.4.wext, bf16[512,512]{1,0:T(8,128)(2,1)} %inverse_upper.1.rinv, bf16[32,256,256]{2,1,0:T(8,128)(2,1)} %lower.3, bf16[32,256,256]{2,1,0:T(8,128)(2,1)} %diag.3, bf16[32,256,256]{2,1,0:T(8,128)(2,1)} %upper.3, ...), custom_call_target="tpu_custom_call" | custom-call | flops 3221225472 | bytes 8388608 | tf_op jit(solution)/shard_map/back/pallas_call | solution.py:451
  164.4 0.0 copy-start
  164.4 3.1 %copy.9 = bf16[8192,128]{1,0:T(8,128)(2,1)} copy(bf16[8192,128]{1,0:T(8,128)(2,1)} %get-tuple-element.8) | data formatting | bytes 4194304
  167.5 0.0 copy-done
  167.5 0.7 copy.10
Async XLA Ops:
  164.4 3.1 %copy-start = (f32[512,128]{1,0:T(8,128)S(1)}, f32[512,128]{1,0:T(8,128)}, u32[]{:S(2)}) copy-start(f32[512,128]{1,0:T(8,128)} %get-tuple-element.9) | copy-start | bytes 786436

commit v2 on v1

--- a/solution.py
+++ b/solution.py
@@ -8,6 +8,7 @@
 from jax.sharding import PartitionSpec as P
 
 LANES = 128
+CHUNK = 2
 MESH = pl.DeviceIdType.MESH
 VMEM = pl.BlockSpec(memory_space=pltpu.VMEM)
 ANY = pl.BlockSpec(memory_space=pl.ANY)
@@ -156,6 +157,19 @@
     return finish
 
 
+def flip(index, bit):
+    return index + bit - 2 * bit * lax.rem(index // bit, 2)
+
+
+def flips(index, mask):
+    bit = 1
+    while bit <= mask:
+        if mask & bit:
+            index = flip(index, bit)
+        bit *= 2
+    return index
+
+
 def apply_block(i, size, field, wl, wd, wu, wi):
     def at(k):
         return field[pl.ds(pl.multiple_of(k * size, size), size), :]
@@ -196,15 +210,18 @@
     def rows(start, extent):
         return pl.ds(pl.multiple_of(start, size), extent)
 
-    spans = ((size, body), (0, size), (top, size))
+    group = CHUNK * size
+    lump = body // group
+    high = lump + 1
+    spans = [(0, size)] + [(size + k * group, group) for k in range(lump)] + [(top, size)]
 
     def landing(kind, k):
         start, extent = spans[kind]
         return field.at[pl.ds(start, extent), columns(k)]
 
     def leaving(kind, d):
-        start, extent = ((d * body, body), (d * body - size, size), (d * body + body, size))[kind]
-        return basis.at[rows(start, extent), :]
+        start, extent = spans[kind]
+        return basis.at[rows(d * body - size + start, extent), :]
 
     def to_peer(step, kind):
         d = lax.rem(c + step, nc)
@@ -215,26 +232,41 @@
 
     def down():
         return remote(
-            basis.at[pl.ds(nc * body - size, size), :], landing(1, c), fsend.at[1, 0], frecv.at[1, c],
+            basis.at[pl.ds(nc * body - size, size), :], landing(0, c), fsend.at[0, 0], frecv.at[0, c],
             rows=r + 1, cols=0,
         )
 
     def up():
         return remote(
-            basis.at[pl.ds(0, size), :], landing(2, c), fsend.at[2, 0], frecv.at[2, c],
+            basis.at[pl.ds(0, size), :], landing(high, c), fsend.at[high, 0], frecv.at[high, c],
             rows=r - 1, cols=nc - 1,
         )
 
+    def each(kind, action):
+        for step in range(1, nc):
+            d = lax.rem(c + step, nc)
+            send = functools.partial(action, step, kind)
+            if kind == 0:
+                pl.when(d > 0)(send)
+            elif kind == high:
+                pl.when(d < nc - 1)(send)
+            else:
+                send()
+
+    def mine_too(kind, action):
+        if kind == 0:
+            pl.when(c > 0)(action)
+        elif kind == high:
+            pl.when(c < nc - 1)(action)
+        else:
+            action()
+
     pl.when(r < nr - 1)(lambda: down().start())
-    pl.when(r > 0)(lambda: up().start())
-    for step in range(1, nc):
-        d = lax.rem(c + step, nc)
-        to_peer(step, 0).start()
-        pl.when(d > 0)(lambda: to_peer(step, 1).start())
-        pl.when(d < nc - 1)(lambda: to_peer(step, 2).start())
-    own(0).start()
-    pl.when(c > 0)(lambda: own(1).start())
-    pl.when(c < nc - 1)(lambda: own(2).start())
+    for kind in range(high + 1):
+        mine_too(kind, lambda: own(kind).start())
+        each(kind, lambda step, kind: to_peer(step, kind).start())
+        if kind == 1:
+            pl.when(r > 0)(lambda: up().start())
 
     @pl.when((r == 0) & (c == 0))
     def _():
@@ -254,23 +286,28 @@
             basis.at[pl.ds(0, extent), :], landing(kind, k), fsend.at[kind, 0], frecv.at[kind, k], cols=k
         ).wait_recv()
 
-    for copy in weights:
-        copy.wait()
-    own(0).wait()
-    pl.when(c > 0)(lambda: own(1).wait())
-    pl.when(c < nc - 1)(lambda: own(2).wait())
-    for k in range(nc):
-        pl.when(k != c)(lambda: arrive(0, k))
-        pl.when(((c > 0) & (k != c)) | ((c == 0) & (r > 0)))(lambda: arrive(1, k))
-        pl.when(((c < nc - 1) & (k != c)) | ((c == nc - 1) & (r < nr - 1)))(lambda: arrive(2, k))
-
     def block(i, carry):
         w = apply_block(i, size, field, wl, wd, wu, wi)
         wext[rows((i + 1) * size, size), :] = w
         total[...] += inner(w, w)
         return carry
 
-    lax.fori_loop(0, count, block, 0)
+    for copy in weights:
+        copy.wait()
+    done = 0
+    for kind in range(high + 1):
+        mine_too(kind, lambda: own(kind).wait())
+        for k in range(nc):
+            comes = k != c
+            if kind == 0:
+                comes = ((c > 0) & comes) | ((c == 0) & (r > 0))
+            elif kind == high:
+                comes = ((c < nc - 1) & comes) | ((c == nc - 1) & (r < nr - 1))
+            pl.when(comes)(lambda: arrive(kind, k))
+        ready = count if kind == high else max(kind * CHUNK - 1, 0)
+        if ready > done:
+            lax.fori_loop(done, ready, block, 0)
+            done = ready
 
     flat = r * nc + c
     last = nr * nc - 1
@@ -303,10 +340,10 @@
         "cols", nc, c, lambda d: tile(packed, d * share, share), lambda k: got1.at[k],
         lambda k: got1.at[k], s1, r1,
     )
+    got1[c] = packed[pl.ds(pl.multiple_of(c * share, 8), share), :]
+    finish()
     pl.when(flat < last)(lambda: halo(0).start())
     pl.when(flat > 0)(lambda: halo(1).start())
-    got1[c] = packed[pl.ds(pl.multiple_of(c * share, 8), share), :]
-    finish()
     part[...] = sum((got1[k] for k in range(1, nc)), got1[0])
     finish = exchange(
         "rows", nr, r, lambda d: tile(part, d * piece, piece), lambda k: got2.at[k],
@@ -331,17 +368,14 @@
     pl.when(flat < last)(lambda: halo(1).wait_recv())
     pl.when(r < nr - 1)(lambda: down().wait_send())
     pl.when(r > 0)(lambda: up().wait_send())
-    for step in range(1, nc):
-        d = lax.rem(c + step, nc)
-        to_peer(step, 0).wait_send()
-        pl.when(d > 0)(lambda: to_peer(step, 1).wait_send())
-        pl.when(d < nc - 1)(lambda: to_peer(step, 2).wait_send())
+    for kind in range(high + 1):
+        each(kind, lambda step, kind: to_peer(step, kind).wait_send())
 
 
 def back_kernel(
     nr, nc, wext, rinv, lower, diag, upper, inverse, ortho, projected,
     oext, wl, wd, wu, wi, total, got1, part, got2,
-    wsem, lsem, osend, orecv, s1, r1, s2, r2, s3, r3,
+    wsem, lsem, osend, orecv, esend, erecv, s1, r1, s2, r2, s3, r3,
 ):
     r, c = lax.axis_index("rows"), lax.axis_index("cols")
     count, size, _ = wl.shape
@@ -360,14 +394,22 @@
 
     lax.fori_loop(0, count + 2, turn, 0)
 
-    def columns(k):
-        return oext.at[pl.ds(size, body), pl.ds(pl.multiple_of(k * width, width), width)]
-
-    def home(k):
-        return ortho.at[pl.ds(pl.multiple_of(k * body, size), body), :]
-
-    finish_ortho = exchange("cols", nc, c, columns, home, home, osend, orecv)
-    own = pltpu.make_async_copy(columns(c), home(c), lsem)
+    early = (count // 2) * size
+
+    def columns(start, extent, k):
+        return oext.at[pl.ds(size + start, extent), pl.ds(pl.multiple_of(k * width, width), width)]
+
+    def home(start, extent, k):
+        return ortho.at[pl.ds(pl.multiple_of(k * body + start, size), extent), :]
+
+    def go_home(start, extent, send, recv):
+        there = functools.partial(home, start, extent)
+        return exchange(
+            "cols", nc, c, functools.partial(columns, start, extent), there, there, send, recv
+        )
+
+    finish_early = go_home(0, early, osend, orecv)
+    own = pltpu.make_async_copy(columns(0, body, c), home(0, body, c), lsem)
     own.start()
     total[...] = jnp.zeros_like(total)
     for copy in weights:
@@ -383,12 +425,31 @@
     def slab(k):
         return pl.ds(pl.multiple_of(k * width, width), width)
 
-    finish = exchange(
-        "cols", nc, c, lambda d: total.at[:, slab(d)], lambda k: got1.at[k], lambda k: got1.at[k], s1, r1
-    )
-    got1[c] = total[:, slab(c)]
-    finish()
-    part[...] = sum((got1[k] for k in range(1, nc)), got1[0])
+    bit, used = 1, 0
+    kept = list(range(0, nc))
+    while bit < nc:
+        peer = flip(c, bit)
+        kept = [k for k in kept if k & bit == 0]
+        copies = [
+            remote(
+                total.at[:, slab(flips(peer, k))], got1.at[used + n], s1.at[used + n], r1.at[used + n],
+                cols=peer,
+            )
+            for n, k in enumerate(kept)
+        ]
+        for copy in copies:
+            copy.start()
+        if 2 * bit == nc:
+            finish_late = go_home(early, body - early, esend, erecv)
+        for n, (k, copy) in enumerate(zip(kept, copies)):
+            copy.wait()
+            where = slab(flips(c, k))
+            if 2 * bit == nc:
+                part[...] = total[:, where] + got1[used + n]
+            else:
+                total[:, where] = total[:, where] + got1[used + n]
+        used += len(kept)
+        bit *= 2
 
     def tile(ref, k):
         return ref.at[pl.ds(pl.multiple_of(k * piece, 8), piece), :]
@@ -406,7 +467,8 @@
         lambda k: tile(projected, k), s3, r3,
     )()
     own.wait()
-    finish_ortho()
+    finish_early()
+    finish_late()
 
 
 def shards(nr, nc, basis, lower, diag, upper, inverse):
@@ -422,6 +484,7 @@
     held = [pltpu.VMEM((count, size, size), jnp.bfloat16)] * 4
     extended = ((count + 2) * size, order)
     pair = lambda n: [dma((n,)), dma((n,))]
+    kinds = count // CHUNK + 2
     opflops = 8 * count * size * size * order + 2 * count * size * order * order
 
     wext, gram = pl.pallas_call(
@@ -438,7 +501,7 @@
             pltpu.VMEM((nc, share, LANES), jnp.float32),
             pltpu.VMEM((share, LANES), jnp.float32),
             pltpu.VMEM((nr, piece, LANES), jnp.float32),
-            dma((4,)), dma((3,)), dma((3, nc)), dma((3, nc)), dma((2,)), dma((2,)),
+            dma((4,)), dma((kinds,)), dma((kinds, nc)), dma((kinds, nc)), dma((2,)), dma((2,)),
         ] + pair(nc) + pair(nr) + pair(nr) + pair(nc),
         compiler_params=pltpu.CompilerParams(has_side_effects=True),
         cost_estimate=pl.CostEstimate(flops=opflops, bytes_accessed=1 << 23, transcendentals=0),
@@ -462,7 +525,7 @@
             pltpu.VMEM((order, width), jnp.float32),
             pltpu.VMEM((nr, lines, width), jnp.float32),
             dma((4,)), dma,
-        ] + pair(nc) + pair(nc) + pair(nr) + pair(nr),
+        ] + pair(nc) + pair(nc) + pair(nc) + pair(nr) + pair(nr),
         compiler_params=pltpu.CompilerParams(has_side_effects=True),
         cost_estimate=pl.CostEstimate(flops=opflops, bytes_accessed=1 << 23, transcendentals=0),
         name="back",

time: 168 us -> 146 us (0.87)
  Pallas kernels: 164 us -> 142 us
    pallas_call x1, Pallas kernels: 60 us -> 44.7 us  [shards(): pl.pallas_call(functools.partial(back_kernel, nr, nc), out_shape=(jax.Sha...]
    pallas_call x1, Pallas kernels: 75.2 us -> 68.5 us  [shards(): pl.pallas_call(functools.partial(front_kernel, nr, nc), out_shape=(jax.Sh...]
where the time goes in v2:
time: 146 us
  Pallas kernels  142 us (97%)
  local copies, waits for them, and re-layouts  3.79 us (3%)
    pallas_call x1, Pallas kernels, shards(): pl.pallas_call(functools.partial(front_kernel, nr, nc), out_shape=(jax.Sh...  68.5 us
    pallas_call x1, Pallas kernels, shards(): pl.pallas_call(functools.partial(back_kernel, nr, nc), out_shape=(jax.Sha...  44.7 us
    pallas_call x1, Pallas kernels, inverse_upper(): pl.pallas_call(unpack_kernel, out_shape=jax.ShapeDtypeStruct((order, orde...  28.6 us
    unnamed x4, local copies, waits for them, and re-layouts  3.79 us

profile of v2, /device:TPU:0, one launch (start us, length us, event | category | flops | bytes accessed | tf_op | source)
XLA Modules:
  0.0 146.2 jit_solution(8914105008563782530)
XLA Ops:
  0.6 68.5 %front.1 = (bf16[2560,512]{1,0:T(8,128)(2,1)}, f32[1280,128]{1,0:T(8,128)}) custom-call(bf16[8192,128]{1,0:T(8,128)(2,1)} %basis.1, bf16[32,256,256]{2,1,0:T(8,128)(2,1)} %lower.3, bf16[32,256,256]{2,1,0:T(8,128)(2,1)} %diag.3, bf16[32,256,256]{2,1,0:T(8,128)(2,1)} %upper.3, bf16[32,256,256]{2,1,0:T(8,128)(2,1)} %inverse.3), custom_call_target="tpu_custom_call" | custom-call | flops 3221225472 | bytes 8388608 | tf_op jit(solution)/shard_map/front/pallas_call | solution.py:490
  69.1 28.6 %inverse_upper.1.rinv = bf16[512,512]{1,0:T(8,128)(2,1)} custom-call(f32[1280,128]{1,0:T(8,128)} %get-tuple-element.5.packed_ref), custom_call_target="tpu_custom_call" | custom-call | flops 1073741824 | bytes 2097152 | tf_op jit(solution)/shard_map/inverse_upper/pallas_call | solution.py:113
  97.7 44.7 %back.1 = (bf16[8192,128]{1,0:T(8,128)(2,1)}, f32[512,128]{1,0:T(8,128)}) custom-call(bf16[2560,512]{1,0:T(8,128)(2,1)} %get-tuple-element.4.wext, bf16[512,512]{1,0:T(8,128)(2,1)} %inverse_upper.1.rinv, bf16[32,256,256]{2,1,0:T(8,128)(2,1)} %lower.3, bf16[32,256,256]{2,1,0:T(8,128)(2,1)} %diag.3, bf16[32,256,256]{2,1,0:T(8,128)(2,1)} %upper.3, ...), custom_call_target="tpu_custom_call" | custom-call | flops 3221225472 | bytes 8388608 | tf_op jit(solution)/shard_map/back/pallas_call | solution.py:514
  142.4 0.0 copy-start
  142.5 3.1 %copy.9 = bf16[8192,128]{1,0:T(8,128)(2,1)} copy(bf16[8192,128]{1,0:T(8,128)(2,1)} %get-tuple-element.8) | data formatting | bytes 4194304
  145.5 0.0 copy-done
  145.5 0.7 copy.10
Async XLA Ops:
  142.4 3.1 %copy-start = (f32[512,128]{1,0:T(8,128)S(1)}, f32[512,128]{1,0:T(8,128)}, u32[]{:S(2)}) copy-start(f32[512,128]{1,0:T(8,128)} %get-tuple-element.9) | copy-start | bytes 786436

commit v3 on v2

--- a/solution.py
+++ b/solution.py
@@ -79,14 +79,21 @@
         for i in range(1, n):
             block = jnp.where(b == i, at[i], block)
         linv = factor_tile(block)
-        y = lax.dot_general(linv, work_ref[b], (((1,), (0,)), ((), ())), precision=HI, preferred_element_type=jnp.float32)
-        work_ref[b] = y
+        live = pl.ds(pl.multiple_of(b * size, size), order + size)
+        work_ref[b, :, live] = lax.dot_general(
+            linv, work_ref[b, :, live], (((1,), (0,)), ((), ())), precision=HI,
+            preferred_element_type=jnp.float32,
+        )
         for i in range(n):
-            panel_ref[i] = y[:, i * size:(i + 1) * size]
+            panel_ref[i] = work_ref[b, :, i * size:(i + 1) * size]
+
         def below(i, c):
-            work_ref[i] = work_ref[i] - lax.dot_general(panel_ref[i], y_ref[...], (((0,), (0,)), ((), ())), precision=HI, preferred_element_type=jnp.float32)
+            work_ref[i, :, live] = work_ref[i, :, live] - lax.dot_general(
+                panel_ref[i], work_ref[b, :, live], (((0,), (0,)), ((), ())), precision=HI,
+                preferred_element_type=jnp.float32,
+            )
             return c
-        y_ref = work_ref.at[b]
+
         lax.fori_loop(b + 1, n, below, 0)
         return carry
     lax.fori_loop(0, n, step, 0)
@@ -392,7 +399,7 @@
         oext[at(i), :] = dot(wext[at(i), :], rinv[...]).astype(jnp.bfloat16)
         return carry
 
-    lax.fori_loop(0, count + 2, turn, 0)
+    lax.fori_loop(0, count // 2 + 1, turn, 0)
 
     early = (count // 2) * size
 
@@ -409,6 +416,7 @@
         )
 
     finish_early = go_home(0, early, osend, orecv)
+    lax.fori_loop(count // 2 + 1, count + 2, turn, 0)
     own = pltpu.make_async_copy(columns(0, body, c), home(0, body, c), lsem)
     own.start()
     total[...] = jnp.zeros_like(total)

time: 146 us -> 142 us (0.973)
  Pallas kernels: 142 us -> 138 us
    pallas_call x1, Pallas kernels: 28.6 us -> 26.4 us  [inverse_upper(): pl.pallas_call(unpack_kernel, out_shape=jax.ShapeDtypeStruct((order, orde...]
    pallas_call x1, Pallas kernels: 44.7 us -> 42.8 us  [shards(): pl.pallas_call(functools.partial(back_kernel, nr, nc), out_shape=(jax.Sha...]
where the time goes in v3:
time: 142 us
  Pallas kernels  138 us (97%)
  local copies, waits for them, and re-layouts  3.79 us (3%)
    pallas_call x1, Pallas kernels, shards(): pl.pallas_call(functools.partial(front_kernel, nr, nc), out_shape=(jax.Sh...  68.5 us
    pallas_call x1, Pallas kernels, shards(): pl.pallas_call(functools.partial(back_kernel, nr, nc), out_shape=(jax.Sha...  42.8 us
    pallas_call x1, Pallas kernels, inverse_upper(): pl.pallas_call(unpack_kernel, out_shape=jax.ShapeDtypeStruct((order, orde...  26.4 us
    unnamed x4, local copies, waits for them, and re-layouts  3.79 us

profile of v3, /device:TPU:0, one launch (start us, length us, event | category | flops | bytes accessed | tf_op | source)
XLA Modules:
  0.0 142.2 jit_solution(18232734924086279538)
XLA Ops:
  0.6 68.5 %front.1 = (bf16[2560,512]{1,0:T(8,128)(2,1)}, f32[1280,128]{1,0:T(8,128)}) custom-call(bf16[8192,128]{1,0:T(8,128)(2,1)} %basis.1, bf16[32,256,256]{2,1,0:T(8,128)(2,1)} %lower.3, bf16[32,256,256]{2,1,0:T(8,128)(2,1)} %diag.3, bf16[32,256,256]{2,1,0:T(8,128)(2,1)} %upper.3, bf16[32,256,256]{2,1,0:T(8,128)(2,1)} %inverse.3), custom_call_target="tpu_custom_call" | custom-call | flops 3221225472 | bytes 8388608 | tf_op jit(solution)/shard_map/front/pallas_call | solution.py:498
  69.1 26.4 %inverse_upper.1.rinv = bf16[512,512]{1,0:T(8,128)(2,1)} custom-call(f32[1280,128]{1,0:T(8,128)} %get-tuple-element.5.packed_ref), custom_call_target="tpu_custom_call" | custom-call | flops 1073741824 | bytes 2097152 | tf_op jit(solution)/shard_map/inverse_upper/pallas_call | solution.py:120
  95.5 42.8 %back.1 = (bf16[8192,128]{1,0:T(8,128)(2,1)}, f32[512,128]{1,0:T(8,128)}) custom-call(bf16[2560,512]{1,0:T(8,128)(2,1)} %get-tuple-element.4.wext, bf16[512,512]{1,0:T(8,128)(2,1)} %inverse_upper.1.rinv, bf16[32,256,256]{2,1,0:T(8,128)(2,1)} %lower.3, bf16[32,256,256]{2,1,0:T(8,128)(2,1)} %diag.3, bf16[32,256,256]{2,1,0:T(8,128)(2,1)} %upper.3, ...), custom_call_target="tpu_custom_call" | custom-call | flops 3221225472 | bytes 8388608 | tf_op jit(solution)/shard_map/back/pallas_call | solution.py:522
  138.4 0.0 copy-start
  138.4 3.1 %copy.9 = bf16[8192,128]{1,0:T(8,128)(2,1)} copy(bf16[8192,128]{1,0:T(8,128)(2,1)} %get-tuple-element.8) | data formatting | bytes 4194304
  141.5 0.0 copy-done
  141.5 0.7 copy.10
Async XLA Ops:
  138.4 3.1 %copy-start = (f32[512,128]{1,0:T(8,128)S(1)}, f32[512,128]{1,0:T(8,128)}, u32[]{:S(2)}) copy-start(f32[512,128]{1,0:T(8,128)} %get-tuple-element.9) | copy-start | bytes 786436
